TPU v7x, 32 devices: a whole 2x2x4 slice. The times are simulated.
32 devices in a mesh: dp: 8 (over z, x), tensor: 4 (over y, core).
Axes of the slice: x: 2, y: 2, z: 4, core: 2. Of those that a mesh axis runs over, the one named last changes fastest.
Arguments:
- tokens: bfloat16 [20480, 768], P(('dp', 'tensor')), may hold values from -6 to 6
- cotangent: bfloat16 [20480, 768], P(('dp', 'tensor')), may hold values from -6 to 6
- lengths: int32 [8, 8], P('dp'), may hold values from 1 to 512, 2048 in all within a row
- w_qkv: bfloat16 [768, 3, 768], P('dp', None, 'tensor'), may hold values from -0.21875 to 0.21875
- w_out: bfloat16 [768, 768], P('tensor', 'dp'), may hold values from -6 to 6
- w_fc: bfloat16 [768, 3072], P('dp', 'tensor'), may hold values from -0.21875 to 0.21875
- w_proj: bfloat16 [3072, 768], P('tensor', 'dp'), may hold values from -0.109375 to 0.109375
- ln1_gain: bfloat16 [768], P('dp'), may hold values from 0.25 to 1.75
- ln1_bias: bfloat16 [768], P('dp'), may hold values from -3 to 3
- ln2_gain: bfloat16 [768], P('dp'), may hold values from 0.25 to 1.75
- ln2_bias: bfloat16 [768], P('dp'), may hold values from -3 to 3
Outputs:
- block_out: bfloat16 [20480, 768], P(('dp', 'tensor'))
- input_grad: bfloat16 [20480, 768], P(('dp', 'tensor'))
- w_qkv_grad: float32 [768, 3, 768], P('dp', None, 'tensor')
- w_out_grad: float32 [768, 768], P('tensor', 'dp')
- w_fc_grad: float32 [768, 3072], P('dp', 'tensor')
- w_proj_grad: float32 [3072, 768], P('tensor', 'dp')
- ln1_gain_grad: float32 [768], P('dp')
- ln1_bias_grad: float32 [768], P('dp')
- ln2_gain_grad: float32 [768], P('dp')
- ln2_bias_grad: float32 [768], P('dp')
Inputs may be any that keep to these rules, and one draw needn't show every extreme that they name: `lengths`: row g lists the token counts of group g's 8 continuations in order after its 512-token prompt; each row sums to 2048 and its largest entry is exactly 512.
All inputs are finite; a program needn't handle non-finite values.
Results may differ from a plain program's by a relative error of at most 0.019.
The roundings to bfloat16 on the way count: a program that leaves them out, or rounds other values in their place, can miss the bound.
Values may be sent and summed in bfloat16 or wider, within the bound.
A program may use at most 192 MiB of HBM per device.

v0:
```python
import jax
import jax.numpy as jnp
from jax import lax
from jax.sharding import PartitionSpec as P

HEAD = 64
PROMPT = 512


def normalize(values):
    mean = jnp.mean(values, axis=-1, keepdims=True)
    centred = values - mean
    spread = jnp.mean(centred * centred, axis=-1, keepdims=True)
    factor = lax.rsqrt(spread + 1e-05)
    return (centred * factor, factor)


def norm_back(grad_out, normed, factor, gain):
    scaled = grad_out * gain
    first = jnp.mean(scaled, axis=-1, keepdims=True)
    second = jnp.mean(scaled * normed, axis=-1, keepdims=True)
    return factor * (scaled - first - normed * second)


def gelu_tanh(values):
    return jax.nn.gelu(values, approximate=True)


def inner_rows(left, right):
    return lax.dot_general(
        left, right, (((0,), (0,)), ((), ())), preferred_element_type=jnp.float32
    )


def times_trans(left, right):
    return lax.dot_general(
        left, right, (((1,), (1,)), ((), ())), preferred_element_type=jnp.float32
    )


def segment_ids(lengths, total):
    ends = PROMPT + jnp.cumsum(lengths[0])
    places = jnp.arange(total, dtype=jnp.int32)
    passed = jnp.sum((places[:, None] >= ends[None, :]).astype(jnp.int32), axis=1)
    return (places, jnp.where(places < PROMPT, -1, passed))


def visible(query_pos, query_seg, key_pos, key_seg):
    causal = key_pos[None, :] <= query_pos[:, None]
    shared = (key_seg[None, :] < 0) | (key_seg[None, :] == query_seg[:, None])
    return (causal & shared)[None]


def attend(queries, keys, values, places, segs, block, scale):
    count = queries.shape[0] // block

    def one(index):
        start = index * block
        query = lax.dynamic_slice_in_dim(queries, start, block, 0)
        mask = visible(
            lax.dynamic_slice_in_dim(places, start, block, 0),
            lax.dynamic_slice_in_dim(segs, start, block, 0),
            places,
            segs,
        )
        raw = jnp.einsum("qhd,khd->hqk", query, keys, preferred_element_type=jnp.float32) * scale
        magnitude = jnp.where(mask, jnp.abs(raw), -1e30)
        top = jnp.max(magnitude, axis=-1, keepdims=True)
        expo = jnp.where(mask, jnp.exp(magnitude - top), 0.0)
        total = jnp.sum(expo, axis=-1, keepdims=True)
        weights = (jnp.sign(raw) * (expo / total)).astype(jnp.bfloat16)
        mixed = jnp.einsum("hqk,khd->qhd", weights, values, preferred_element_type=jnp.float32)
        return (mixed.astype(jnp.bfloat16), (top + jnp.log(total))[..., 0])

    mixed, sums = lax.map(one, jnp.arange(count, dtype=jnp.int32))
    return (mixed.reshape(queries.shape[0], -1), sums)


def attend_back(queries, keys, values, grad_mixed, sums, places, segs, block, scale):
    count = queries.shape[0] // block

    def step(carry, inputs):
        key_grad, value_grad = carry
        index, lse_block = inputs
        start = index * block
        query = lax.dynamic_slice_in_dim(queries, start, block, 0)
        grad_block = lax.dynamic_slice_in_dim(grad_mixed, start, block, 0)
        mask = visible(
            lax.dynamic_slice_in_dim(places, start, block, 0),
            lax.dynamic_slice_in_dim(segs, start, block, 0),
            places,
            segs,
        )
        raw = jnp.einsum("qhd,khd->hqk", query, keys, preferred_element_type=jnp.float32) * scale
        prob = jnp.where(mask, jnp.exp(jnp.abs(raw) - lse_block[..., None]), 0.0)
        signed = jnp.sign(raw) * prob
        rounded = signed.astype(jnp.bfloat16)
        value_grad = value_grad + jnp.einsum(
            "hqk,qhd->khd", rounded, grad_block, preferred_element_type=jnp.float32
        )
        weight_grad = jnp.einsum(
            "qhd,khd->hqk", grad_block, values, preferred_element_type=jnp.float32
        )
        inner = jnp.sum(signed * weight_grad, axis=-1, keepdims=True)
        score_grad = (prob * weight_grad - signed * inner).astype(jnp.bfloat16)
        query_grad = (
            jnp.einsum("hqk,khd->qhd", score_grad, keys, preferred_element_type=jnp.float32) * scale
        )
        key_grad = (
            key_grad
            + jnp.einsum("hqk,qhd->khd", score_grad, query, preferred_element_type=jnp.float32)
            * scale
        )
        return ((key_grad, value_grad), query_grad)

    zeros = jnp.zeros(keys.shape, jnp.float32)
    (key_grad, value_grad), query_grad = lax.scan(
        step, (zeros, zeros), (jnp.arange(count, dtype=jnp.int32), sums)
    )
    return (query_grad.reshape(keys.shape), key_grad, value_grad)


def on_device(
    tokens, cotangent, lengths, w_qkv, w_out, w_fc, w_proj, ln1_gain, ln1_bias, ln2_gain, ln2_bias
):
    rows = tokens.shape[0]
    group = rows * lax.axis_size("tensor")
    block = group // max(1, group // 512)
    scale = HEAD ** (-0.5)
    pieces = (w_qkv, w_out, w_fc, w_proj, ln1_gain, ln1_bias, ln2_gain, ln2_bias)
    qkv_full, out_full, fc_full, proj_full, gain1, bias1, gain2, bias2 = (
        lax.all_gather(pieces[0], "dp", axis=0, tiled=True),
        lax.all_gather(pieces[1], "dp", axis=1, tiled=True),
        lax.all_gather(pieces[2], "dp", axis=0, tiled=True),
        lax.all_gather(pieces[3], "dp", axis=1, tiled=True),
        lax.all_gather(pieces[4], "dp", axis=0, tiled=True),
        lax.all_gather(pieces[5], "dp", axis=0, tiled=True),
        lax.all_gather(pieces[6], "dp", axis=0, tiled=True),
        lax.all_gather(pieces[7], "dp", axis=0, tiled=True),
    )
    gain1 = gain1.astype(jnp.float32)
    bias1 = bias1.astype(jnp.float32)
    gain2 = gain2.astype(jnp.float32)
    bias2 = bias2.astype(jnp.float32)
    width = qkv_full.shape[0]
    local = qkv_full.shape[2]
    heads = local // HEAD
    qkv_mat = qkv_full.reshape(width, 3 * local)
    places, segs = segment_ids(lengths, group)
    inputs = tokens.astype(jnp.float32)
    normed1, factor1 = normalize(inputs)
    lowered1 = (normed1 * gain1 + bias1).astype(jnp.bfloat16)
    all_norm1 = lax.all_gather(lowered1, "tensor", axis=0, tiled=True)
    projected = jnp.dot(all_norm1, qkv_mat, preferred_element_type=jnp.float32).astype(jnp.bfloat16)
    projected = projected.reshape(group, 3, heads, HEAD)
    queries = projected[:, 0]
    keys = projected[:, 1]
    values = projected[:, 2]
    mixed, sums = attend(queries, keys, values, places, segs, block, scale)
    part = mixed
    resid = inputs + lax.psum_scatter(
        jnp.dot(part, out_full, preferred_element_type=jnp.float32).astype(jnp.bfloat16),
        "tensor",
        scatter_dimension=0,
        tiled=True,
    ).astype(jnp.float32)
    normed2, factor2 = normalize(resid)
    lowered2 = (normed2 * gain2 + bias2).astype(jnp.bfloat16)
    all_norm2 = lax.all_gather(lowered2, "tensor", axis=0, tiled=True)
    hidden_pre = jnp.dot(all_norm2, fc_full, preferred_element_type=jnp.float32)
    hidden, gelu_pull = jax.vjp(gelu_tanh, hidden_pre)
    hidden_low = hidden.astype(jnp.bfloat16)
    part = hidden_low
    mlp_rows = lax.psum_scatter(
        jnp.dot(part, proj_full, preferred_element_type=jnp.float32).astype(jnp.bfloat16),
        "tensor",
        scatter_dimension=0,
        tiled=True,
    ).astype(jnp.float32)
    block_out = (resid + mlp_rows).astype(jnp.bfloat16)
    grad_all = lax.all_gather(cotangent, "tensor", axis=0, tiled=True)
    hidden_grad = times_trans(grad_all, proj_full)
    proj_grad = inner_rows(hidden_low, grad_all)
    pre_low = gelu_pull(hidden_grad)[0].astype(jnp.bfloat16)
    fc_grad = inner_rows(all_norm2, pre_low)
    part = pre_low
    norm2_grad = lax.psum_scatter(
        times_trans(part, fc_full).astype(jnp.bfloat16), "tensor", scatter_dimension=0, tiled=True
    ).astype(jnp.float32)
    gain2_part = jnp.sum(norm2_grad * normed2, axis=0)
    bias2_part = jnp.sum(norm2_grad, axis=0)
    resid_grad = cotangent.astype(jnp.float32) + norm_back(norm2_grad, normed2, factor2, gain2)
    resid_low = resid_grad.astype(jnp.bfloat16)
    resid_all = lax.all_gather(resid_low, "tensor", axis=0, tiled=True)
    out_grad = inner_rows(mixed, resid_all)
    mixed_grad = times_trans(resid_all, out_full).astype(jnp.bfloat16).reshape(group, heads, HEAD)
    query_grad, key_grad, value_grad = attend_back(
        queries, keys, values, mixed_grad, sums, places, segs, block, scale
    )
    qkv_grad_low = (
        jnp.stack([query_grad, key_grad, value_grad], axis=1)
        .astype(jnp.bfloat16)
        .reshape(group, 3 * local)
    )
    qkv_grad = inner_rows(all_norm1, qkv_grad_low).reshape(width, 3, local)
    part = qkv_grad_low
    norm1_grad = lax.psum_scatter(
        times_trans(part, qkv_mat).astype(jnp.bfloat16), "tensor", scatter_dimension=0, tiled=True
    ).astype(jnp.float32)
    gain1_part = jnp.sum(norm1_grad * normed1, axis=0)
    bias1_part = jnp.sum(norm1_grad, axis=0)
    input_grad = (resid_grad + norm_back(norm1_grad, normed1, factor1, gain1)).astype(jnp.bfloat16)
    qkv_sum, out_sum, fc_sum, proj_sum, gain1_share, bias1_share, gain2_share, bias2_share = (
        lax.psum_scatter(qkv_grad, "dp", scatter_dimension=0, tiled=True),
        lax.psum_scatter(out_grad, "dp", scatter_dimension=1, tiled=True),
        lax.psum_scatter(fc_grad, "dp", scatter_dimension=0, tiled=True),
        lax.psum_scatter(proj_grad, "dp", scatter_dimension=1, tiled=True),
        lax.psum_scatter(gain1_part, "dp", scatter_dimension=0, tiled=True),
        lax.psum_scatter(bias1_part, "dp", scatter_dimension=0, tiled=True),
        lax.psum_scatter(gain2_part, "dp", scatter_dimension=0, tiled=True),
        lax.psum_scatter(bias2_part, "dp", scatter_dimension=0, tiled=True),
    )
    gain1_sum, bias1_sum, gain2_sum, bias2_sum = lax.psum(
        (gain1_share, bias1_share, gain2_share, bias2_share), "tensor"
    )
    return (
        block_out,
        input_grad,
        qkv_sum,
        out_sum,
        fc_sum,
        proj_sum,
        gain1_sum,
        bias1_sum,
        gain2_sum,
        bias2_sum,
    )


def solution(mesh):
    placed = (
        P(("dp", "tensor"), None),
        P(("dp", "tensor"), None),
        P("dp", None),
        P("dp", None, "tensor"),
        P("tensor", "dp"),
        P("dp", "tensor"),
        P("tensor", "dp"),
        P("dp"),
        P("dp"),
        P("dp"),
        P("dp"),
    )
    return jax.shard_map(
        on_device,
        mesh=mesh,
        in_specs=placed,
        out_specs=(
            P(("dp", "tensor"), None),
            P(("dp", "tensor"), None),
            P("dp", None, "tensor"),
            P("tensor", "dp"),
            P("dp", "tensor"),
            P("tensor", "dp"),
            P("dp"),
            P("dp"),
            P("dp"),
            P("dp"),
        ),
        check_vma=False,
    )
```

profile of v0, /device:TPU:0, one launch (start us, length us, event | category | flops | bytes accessed | tf_op | source)
XLA Modules:
  0.0 1164.4 jit_solution(4583404668944278764)
XLA Ops:
  13.4 23.9 %all-reduce.10 = (bf16[768]{0:T(1024)(128)(2,1)}, bf16[768]{0:T(1024)(128)(2,1)}, bf16[768]{0:T(1024)(128)(2,1)S(1)}, bf16[768]{0:T(1024)(128)(2,1)S(1)}) all-reduce(bf16[768]{0:T(1024)(128)(2,1)S(1)} %dynamic-update-slice.3, bf16[768]{0:T(1024)(128)(2,1)S(1)} %dynamic-update-slice.2, ...), channel_id=1, replica_groups=mesh['dp'=8,'tensor'=4] {'dp'}, use_global_device_ids=true, to_apply=%add.3 | all-reduce | flops 3072 | bytes 12288
  43.6 35.5 %all_gather.39 = bf16[768,3,192]{2,1,0:T(4,128)(2,1)S(1)} all-gather(bf16[96,3,192]{2,1,0:T(4,128)(2,1)S(1)} %copy.32), channel_id=1, replica_groups=mesh['dp'=8,'tensor'=4] {'dp'}, dimensions={0}, use_global_device_ids=true | all-gather | bytes 995328 | tf_op jit(solution)/shard_map/all_gather | solution.py:132
  80.1 33.6 %all_gather.40 = bf16[192,768]{0,1:T(8,128)(2,1)} all-gather(bf16[192,96]{0,1:T(8,128)(2,1)S(1)} %copy.35), channel_id=1, replica_groups=mesh['dp'=8,'tensor'=4] {'dp'}, dimensions={1}, use_global_device_ids=true | all-gather | bytes 331776 | tf_op jit(solution)/shard_map/all_gather | solution.py:133
  119.7 122.1 %while.29 = (s32[]{:T(128)}, bf16[5,512,3,64]{1,3,2,0:T(8,128)(2,1)S(1)}, f32[5,3,512]{2,1,0:T(4,128)S(1)}, s32[5]{0:T(128)S(1)}, bf16[2560,3,64]{0,2,1:T(8,128)...) while((s32[]{:T(128)}, ...), condition=%wide.region_7.8_spmd.clone, body=%wide.region_4.7_spmd.clone.sunk | while | flops 1086686208 | bytes 54895824 | solution.py:75
  248.8 40.7 %reduce-scatter.11.cloned.1.call-done = bf16[640,768]{1,0:T(8,128)(2,1)} async-done(((bf16[2560,768]{1,0:T(8,128)(2,1)}), bf16[640,768]{1,0:T(8,128)(2,1)}) %reduce-scatter.11.cloned.1.call-update) | async-done | bytes 983056 | tf_op jit(solution)/shard_map/reduce_scatter | solution.py:161
  294.4 28.8 %all-gather.15.cloned.1.call-done = bf16[2560,768]{1,0:T(8,128)(2,1)} async-done(((bf16[640,768]{1,0:T(8,128)(2,1)}), bf16[2560,768]{1,0:T(8,128)(2,1)}) %all-gather.15.cloned.1.call-update) | async-done | bytes 3932176 | tf_op jit(solution)/shard_map/all_gather | solution.py:181
  332.1 34.7 %all-gather.11.cloned.1.call-done = bf16[768,768]{1,0:T(8,128)(2,1)} async-done(((bf16[96,768]{1,0:T(8,128)(2,1)}), bf16[768,768]{1,0:T(8,128)(2,1)}) %all-gather.11.cloned.1.call-update) | async-done | bytes 1179664 | tf_op jit(solution)/shard_map/all_gather | solution.py:134
  366.7 33.4 %all-gather.9.cloned.1.call-done = bf16[2560,768]{1,0:T(8,128)(2,1)} async-done(((bf16[640,768]{1,0:T(8,128)(2,1)}), bf16[2560,768]{1,0:T(8,128)(2,1)}) %all-gather.9.cloned.1.call-update) | async-done | bytes 3932176 | tf_op jit(solution)/shard_map/all_gather | solution.py:169
  421.0 42.6 %reduce-scatter.15.cloned.1.call-done = bf16[640,768]{1,0:T(8,128)(2,1)} async-done(((bf16[2560,768]{1,0:T(8,128)(2,1)}), bf16[640,768]{1,0:T(8,128)(2,1)}) %reduce-scatter.15.cloned.1.call-update) | async-done | bytes 983056 | tf_op jit(solution)/shard_map/reduce_scatter | solution.py:187
  470.5 32.9 %all-gather.17.cloned.1.call-done = bf16[2560,768]{1,0:T(8,128)(2,1)} async-done(((bf16[640,768]{1,0:T(8,128)(2,1)}), bf16[2560,768]{1,0:T(8,128)(2,1)}) %all-gather.17.cloned.1.call-update) | async-done | bytes 3932176 | tf_op jit(solution)/shard_map/all_gather | solution.py:194
  512.9 323.7 %while.30 = (s32[]{:T(128)}, f32[2560,3,64]{0,2,1:T(8,128)}, f32[2560,3,64]{0,2,1:T(8,128)}, bf16[5,512,3,64]{1,0,3,2:T(8,128)(2,1)}, s32[5]{0:T(128)S(1)}, /*in...) while((s32[]{:T(128)}, f32[2560,3,64]{0,2,1:T(8,128)}, ...), condition=%wide.region_17.18_spmd.clone.clone, body=%wide.region_15.17_spmd.clone.clone.sunk | while | flops 2622784512 | bytes 218457456 | solution.py:117
  531.7 15.0 %multiply_reduce_fusion.3 = (f32[3,512]{1,0:T(4,128)S(1)}, f32[3,512,2560]{2,1,0:T(8,128)}) fusion(f32[3,512,2560]{2,1,0:T(8,128)S(1)} %fusion.137, f32[3,512]{1,0:T(4,128)S(1)} %dynamic-slice_bitcast_fusion.2, pred[512,2560]{1,0:T(8,128)(4,1)S(1)} %or_and_fusion.5, bf16[2560,3,64]{0,2,1:T(8,128)(2,1)S(1)} %copy-done.12, ...), kind=kOutput, calls=%fused_computation.19.clone.1 | convolution fusion | flops 534772224 | bytes 33959940 | tf_op jit(solution)/shard_map/while/body/eval_jaxpr/qhd,khd->hqk/dot_general | solution.py:101
  546.7 15.2 %subtract_convert_fusion.2 = bf16[3,512,2560]{2,1,0:T(8,128)(2,1)S(1)} fusion(f32[3,512,2560]{2,1,0:T(8,128)} %get-tuple-element.433, f32[3,512,2560]{2,1,0:T(8,128)} %copy-done, f32[3,512]{1,0:T(4,128)S(1)} %get-tuple-element.434, f32[3,512]{1,0:T(4,128)S(1)} %dynamic-slice_bitcast_fusion.2, pred[512,2560]{1,0:T(8,128)(4,1)S(1)} %or_and_fusion.5), kind=kLoop, calls=%fused_computation.18.clone.1 | loop fusion | flops 39321600 | bytes 40644608 | tf_op jit(solution)/shard_map/while/body/eval_jaxpr/convert_element_type | solution.py:105
  611.8 15.2 %subtract_convert_fusion.2 = bf16[3,512,2560]{2,1,0:T(8,128)(2,1)S(1)} fusion(f32[3,512,2560]{2,1,0:T(8,128)} %get-tuple-element.433, f32[3,512,2560]{2,1,0:T(8,128)} %copy-done, f32[3,512]{1,0:T(4,128)S(1)} %get-tuple-element.434, f32[3,512]{1,0:T(4,128)S(1)} %dynamic-slice_bitcast_fusion.2, pred[512,2560]{1,0:T(8,128)(4,1)S(1)} %or_and_fusion.5), kind=kLoop, calls=%fused_computation.18.clone.1 | loop fusion | flops 39321600 | bytes 40644608 | tf_op jit(solution)/shard_map/while/body/eval_jaxpr/convert_element_type | solution.py:105
  661.8 15.0 %multiply_reduce_fusion.3 = (f32[3,512]{1,0:T(4,128)S(1)}, f32[3,512,2560]{2,1,0:T(8,128)}) fusion(f32[3,512,2560]{2,1,0:T(8,128)S(1)} %fusion.137, f32[3,512]{1,0:T(4,128)S(1)} %dynamic-slice_bitcast_fusion.2, pred[512,2560]{1,0:T(8,128)(4,1)S(1)} %or_and_fusion.5, bf16[2560,3,64]{0,2,1:T(8,128)(2,1)S(1)} %copy-done.12, ...), kind=kOutput, calls=%fused_computation.19.clone.1 | convolution fusion | flops 534772224 | bytes 33959940 | tf_op jit(solution)/shard_map/while/body/eval_jaxpr/qhd,khd->hqk/dot_general | solution.py:101
  676.8 15.2 %subtract_convert_fusion.2 = bf16[3,512,2560]{2,1,0:T(8,128)(2,1)S(1)} fusion(f32[3,512,2560]{2,1,0:T(8,128)} %get-tuple-element.433, f32[3,512,2560]{2,1,0:T(8,128)} %copy-done, f32[3,512]{1,0:T(4,128)S(1)} %get-tuple-element.434, f32[3,512]{1,0:T(4,128)S(1)} %dynamic-slice_bitcast_fusion.2, pred[512,2560]{1,0:T(8,128)(4,1)S(1)} %or_and_fusion.5), kind=kLoop, calls=%fused_computation.18.clone.1 | loop fusion | flops 39321600 | bytes 40644608 | tf_op jit(solution)/shard_map/while/body/eval_jaxpr/convert_element_type | solution.py:105
  726.9 15.0 %multiply_reduce_fusion.3 = (f32[3,512]{1,0:T(4,128)S(1)}, f32[3,512,2560]{2,1,0:T(8,128)}) fusion(f32[3,512,2560]{2,1,0:T(8,128)S(1)} %fusion.137, f32[3,512]{1,0:T(4,128)S(1)} %dynamic-slice_bitcast_fusion.2, pred[512,2560]{1,0:T(8,128)(4,1)S(1)} %or_and_fusion.5, bf16[2560,3,64]{0,2,1:T(8,128)(2,1)S(1)} %copy-done.12, ...), kind=kOutput, calls=%fused_computation.19.clone.1 | convolution fusion | flops 534772224 | bytes 33959940 | tf_op jit(solution)/shard_map/while/body/eval_jaxpr/qhd,khd->hqk/dot_general | solution.py:101
  741.9 15.2 %subtract_convert_fusion.2 = bf16[3,512,2560]{2,1,0:T(8,128)(2,1)S(1)} fusion(f32[3,512,2560]{2,1,0:T(8,128)} %get-tuple-element.433, f32[3,512,2560]{2,1,0:T(8,128)} %copy-done, f32[3,512]{1,0:T(4,128)S(1)} %get-tuple-element.434, f32[3,512]{1,0:T(4,128)S(1)} %dynamic-slice_bitcast_fusion.2, pred[512,2560]{1,0:T(8,128)(4,1)S(1)} %or_and_fusion.5), kind=kLoop, calls=%fused_computation.18.clone.1 | loop fusion | flops 39321600 | bytes 40644608 | tf_op jit(solution)/shard_map/while/body/eval_jaxpr/convert_element_type | solution.py:105
  792.0 15.0 %multiply_reduce_fusion.3 = (f32[3,512]{1,0:T(4,128)S(1)}, f32[3,512,2560]{2,1,0:T(8,128)}) fusion(f32[3,512,2560]{2,1,0:T(8,128)S(1)} %fusion.137, f32[3,512]{1,0:T(4,128)S(1)} %dynamic-slice_bitcast_fusion.2, pred[512,2560]{1,0:T(8,128)(4,1)S(1)} %or_and_fusion.5, bf16[2560,3,64]{0,2,1:T(8,128)(2,1)S(1)} %copy-done.12, ...), kind=kOutput, calls=%fused_computation.19.clone.1 | convolution fusion | flops 534772224 | bytes 33959940 | tf_op jit(solution)/shard_map/while/body/eval_jaxpr/qhd,khd->hqk/dot_general | solution.py:101
  807.0 15.2 %subtract_convert_fusion.2 = bf16[3,512,2560]{2,1,0:T(8,128)(2,1)S(1)} fusion(f32[3,512,2560]{2,1,0:T(8,128)} %get-tuple-element.433, f32[3,512,2560]{2,1,0:T(8,128)} %copy-done, f32[3,512]{1,0:T(4,128)S(1)} %get-tuple-element.434, f32[3,512]{1,0:T(4,128)S(1)} %dynamic-slice_bitcast_fusion.2, pred[512,2560]{1,0:T(8,128)(4,1)S(1)} %or_and_fusion.5), kind=kLoop, calls=%fused_computation.18.clone.1 | loop fusion | flops 39321600 | bytes 40644608 | tf_op jit(solution)/shard_map/while/body/eval_jaxpr/convert_element_type | solution.py:105
  893.8 37.1 %all-reduce.8 = (f32[768]{0:T(1024)S(1)}, f32[768]{0:T(1024)S(1)}, f32[768]{0:T(1024)S(1)}, f32[768]{0:T(1024)S(1)}) all-reduce(f32[768]{0:T(1024)S(1)} %get-tuple-element.224, f32[768]{0:T(1024)S(1)} %get-tuple-element.229, f32[768]{0:T(1024)S(1)} %copy-done.34, ...), channel_id=10, replica_groups=mesh['dp'=8,'tensor'=4] {'dp'}, use_global_device_ids=true, to_apply=%region_26.27.clone | all-reduce | flops 3072 | bytes 24576
  941.8 68.8 %reduce-scatter.21.cloned.1.call-done = f32[96,768]{1,0:T(8,128)} async-done(((f32[768,768]{1,0:T(8,128)}), f32[96,768]{1,0:T(8,128)}) %reduce-scatter.21.cloned.1.call-update) | async-done | bytes 294928 | tf_op jit(solution)/shard_map/reduce_scatter | solution.py:216
  1010.6 73.1 %reduce-scatter.23.cloned.1.call-done = f32[768,96]{0,1:T(8,128)} async-done(((f32[768,768]{0,1:T(8,128)}), f32[768,96]{0,1:T(8,128)}) %reduce-scatter.23.cloned.1.call-update) | async-done | bytes 294928 | tf_op jit(solution)/shard_map/reduce_scatter | solution.py:217
  1083.8 73.1 %reduce-scatter.19.cloned.1.call-done = f32[96,3,192]{2,0,1:T(8,128)} async-done(((f32[768,3,192]{2,0,1:T(8,128)}), f32[96,3,192]{2,0,1:T(8,128)}) %reduce-scatter.19.cloned.1.call-update) | async-done | bytes 221200 | tf_op jit(solution)/shard_map/reduce_scatter | solution.py:214
  (324 shorter events, 444.4 us)
Async XLA Ops:
  8.0 105.7 %all-gather.7.cloned.1.call-start = ((), (), s32[]{:S(2)}) async-start(), calls=%async_computation.8 | async-start | bytes 4915200 | tf_op jit(solution)/shard_map/all_gather | solution.py:153
  43.0 246.5 %reduce-scatter.11.cloned.1.call-start = ((), (), s32[]{:S(2)}) async-start(), calls=%async_computation.9 | async-start | bytes 4915200 | tf_op jit(solution)/shard_map/reduce_scatter | solution.py:161
  247.0 47.5 %all-gather.13.cloned.1.call-start = ((), (), s32[]{:S(2)}) async-start(), calls=%async_computation.12 | async-start | bytes 1327104 | tf_op jit(solution)/shard_map/all_gather | solution.py:135
  247.5 75.7 %all-gather.15.cloned.1.call-start = ((), (), s32[]{:S(2)}) async-start(), calls=%async_computation.14 | async-start | bytes 4915200 | tf_op jit(solution)/shard_map/all_gather | solution.py:181
  248.1 118.6 %all-gather.11.cloned.1.call-start = ((), (), s32[]{:S(2)}) async-start(), calls=%async_computation.11 | async-start | bytes 1327104 | tf_op jit(solution)/shard_map/all_gather | solution.py:134
  248.7 151.4 %all-gather.9.cloned.1.call-start = ((), (), s32[]{:S(2)}) async-start(), calls=%async_computation.10 | async-start | bytes 4915200 | tf_op jit(solution)/shard_map/all_gather | solution.py:169
  248.8 217.6 %copy-start.21 = (f32[768]{0:T(1024)}, f32[768]{0:T(1024)S(1)}, u32[]{:S(2)}) copy-start(f32[768]{0:T(1024)S(1)} %convert_element_type.109) | copy-start | bytes 9220
  291.2 175.2 %copy-start.17 = (f32[640]{0:T(1024)}, f32[640]{0:T(1024)S(1)}, u32[]{:S(2)}) copy-start(f32[640]{0:T(1024)S(1)} %broadcast_multiply_fusion.4) | copy-start | bytes 7684
  292.9 173.5 %copy-start.23 = (f32[640]{0:T(1024)}, f32[640]{0:T(1024)S(1)}, u32[]{:S(2)}) copy-start(f32[640]{0:T(1024)S(1)} %add_rsqrt_fusion) | copy-start | bytes 7684
  294.4 169.2 %reduce-scatter.15.cloned.1.call-start = ((), (), s32[]{:S(2)}) async-start(), calls=%async_computation.15 | async-start | bytes 4915200 | tf_op jit(solution)/shard_map/reduce_scatter | solution.py:187
  420.5 82.9 %all-gather.17.cloned.1.call-start = ((), (), s32[]{:S(2)}) async-start(), calls=%async_computation.16 | async-start | bytes 4915200 | tf_op jit(solution)/shard_map/all_gather | solution.py:194
  470.4 416.2 %reduce-scatter.25.cloned.1.call-start = ((), (), s32[]{:S(2)}) async-start(), calls=%async_computation.21 | async-start | bytes 884736
  508.3 383.3 %reduce-scatter.17.cloned.1.call-start = ((), (), s32[]{:S(2)}) async-start(), calls=%async_computation.17 | async-start | bytes 4915200 | tf_op jit(solution)/shard_map/reduce_scatter | solution.py:207
  848.7 88.9 %reduce-scatter.13.cloned.1.call-start = ((), (), s32[]{:S(2)}) async-start(), calls=%async_computation.13 | async-start | bytes 4915200 | tf_op jit(solution)/shard_map/reduce_scatter | solution.py:174
  859.8 150.8 %reduce-scatter.21.cloned.1.call-start = ((), (), s32[]{:S(2)}) async-start(), calls=%async_computation.19 | async-start | bytes 2654208 | tf_op jit(solution)/shard_map/reduce_scatter | solution.py:216
  868.0 215.8 %reduce-scatter.23.cloned.1.call-start = ((), (), s32[]{:S(2)}) async-start(), calls=%async_computation.20 | async-start | bytes 2654208 | tf_op jit(solution)/shard_map/reduce_scatter | solution.py:217
  877.8 279.1 %reduce-scatter.19.cloned.1.call-start = ((), (), s32[]{:S(2)}) async-start(), calls=%async_computation.18 | async-start | bytes 2654208 | tf_op jit(solution)/shard_map/reduce_scatter | solution.py:214
  885.7 51.9 %copy-start.6 = (bf16[640,768]{1,0:T(8,128)(2,1)S(1)}, bf16[640,768]{1,0:T(8,128)(2,1)}, u32[]{:S(2)}) copy-start(bf16[640,768]{1,0:T(8,128)(2,1)} %reduce-scatter.11.cloned.1.call-done) | copy-start | bytes 2949124
  885.7 51.9 %copy-start.7 = (bf16[640,768]{1,0:T(8,128)(2,1)S(1)}, bf16[640,768]{1,0:T(8,128)(2,1)}, u32[]{:S(2)}) copy-start(bf16[640,768]{1,0:T(8,128)(2,1)} %param.16) | copy-start | bytes 2949124
  885.7 51.9 %copy-start.18 = (f32[640]{0:T(1024)S(1)}, f32[640]{0:T(1024)}, u32[]{:S(2)}) copy-start(f32[640]{0:T(1024)} %copy-done.17) | copy-start | bytes 7684
  885.7 51.9 %copy-start.22 = (f32[768]{0:T(1024)S(1)}, f32[768]{0:T(1024)}, u32[]{:S(2)}) copy-start(f32[768]{0:T(1024)} %copy-done.21) | copy-start | bytes 9220
  885.7 51.9 %copy-start.24 = (f32[640]{0:T(1024)S(1)}, f32[640]{0:T(1024)}, u32[]{:S(2)}) copy-start(f32[640]{0:T(1024)} %copy-done.23) | copy-start | bytes 7684
  885.7 51.9 %copy-start.31 = (f32[640]{0:T(1024)S(1)}, f32[640]{0:T(1024)}, u32[]{:S(2)}) copy-start(f32[640]{0:T(1024)} %copy-done.30) | copy-start | bytes 7684
  885.7 51.9 %copy-start.33 = (f32[640]{0:T(1024)S(1)}, f32[640]{0:T(1024)}, u32[]{:S(2)}) copy-start(f32[640]{0:T(1024)} %copy-done.32) | copy-start | bytes 7684
  (48 other events, 506.7 us)
Sparse Core Ops, SparseCore 0:
  43.1 30.2 all-gather.6
  247.1 42.4 reduce-scatter.10
  420.6 42.8 reduce-scatter.14
Sparse Core Ops, SparseCore 1:
  249.6 40.9 all-gather.12
  292.0 31.2 all-gather.14
  325.3 41.4 all-gather.10
  368.9 31.2 all-gather.8
  470.5 32.8 all-gather.16
  508.4 63.3 reduce-scatter.24
  848.7 42.8 reduce-scatter.16
  894.0 42.8 reduce-scatter.12
  940.8 69.8 reduce-scatter.20
  1014.7 69.0 reduce-scatter.22
  1087.7 69.1 reduce-scatter.18
where the time goes:
time: 1170 us; the launch traced here: 1160 us
  waiting for transfers between devices  433 us (37%)
  matrix products  348 us (30%)
  other arithmetic  148 us (13%)
  blocking collectives  137 us (12%)
  local copies, waits for them, and re-layouts  71.7 us (6%)
  between operations  17.7 us (2%)
    convert_element_type x5, other arithmetic, step(): score_grad = (prob * weight_grad - signed * inner).astype(jnp.bfloat16)  76.2 us
    dot_general x5, matrix products, step(): jnp.einsum('qhd,khd->hqk', grad_block, values, preferred_element_type=jnp...  75 us
    reduce_scatter x1, waiting for transfers between devices, on_device(): lax.psum_scatter(qkv_grad, 'dp', scatter_dimension=0, tiled=True)  73.1 us
    reduce_scatter x1, waiting for transfers between devices, on_device(): lax.psum_scatter(proj_grad, 'dp', scatter_dimension=1, tiled=True)  73.1 us
    dot_general x5, matrix products, step(): jnp.einsum('hqk,qhd->khd', rounded, grad_block, preferred_element_type=jn...  69.8 us
    reduce_scatter x1, waiting for transfers between devices, on_device(): lax.psum_scatter(fc_grad, 'dp', scatter_dimension=0, tiled=True)  68.8 us
    unnamed x2, blocking collectives  61 us
    dot_general x5, matrix products, one(): jnp.einsum('hqk,khd->qhd', weights, values, preferred_element_type=jnp.fl...  52.9 us
  transfers between devices with their start and end apart: 14, of which 10 were waited for; matrix products, arithmetic and copies ran while one was open for 34% of the time, Pallas kernels for 0%

commit v1 on v0

--- a/solution.py
+++ b/solution.py
@@ -1,10 +1,38 @@
+import functools
 import jax
 import jax.numpy as jnp
 from jax import lax
 from jax.sharding import PartitionSpec as P
+from jax.lax import axis_index, axis_size, ppermute
 
 HEAD = 64
 PROMPT = 512
+
+
+def pair_frames(u, dim_i):
+    u = jnp.moveaxis(u, 0, dim_i)
+    e_next = u.shape
+    return u.reshape(*e_next[:dim_i], e_next[dim_i] * e_next[dim_i + 1], *e_next[dim_i + 2 :])
+
+
+def build_digits(frame, named_axis):
+    v_next, even = (axis_size(named_axis), axis_index(named_axis))
+    res, x_now = (frame[None], 1)
+    while x_now < v_next:
+        piece_next = ppermute(
+            res, axis_name=named_axis, perm=[(dev, dev ^ x_now) for dev in range(v_next)]
+        )
+        u1 = even & x_now == 0
+        res = jnp.concatenate([jnp.where(u1, res, piece_next), jnp.where(u1, piece_next, res)])
+        x_now *= 2
+    return res
+
+
+def rest_the_frame(packet, payload, out_dim):
+    return pair_frames(build_digits(packet, payload), out_dim)
+
+
+paths_refer = functools.partial(rest_the_frame, payload="dp", out_dim=1)
 
 
 def normalize(values):
@@ -130,7 +158,7 @@
     pieces = (w_qkv, w_out, w_fc, w_proj, ln1_gain, ln1_bias, ln2_gain, ln2_bias)
     qkv_full, out_full, fc_full, proj_full, gain1, bias1, gain2, bias2 = (
         lax.all_gather(pieces[0], "dp", axis=0, tiled=True),
-        lax.all_gather(pieces[1], "dp", axis=1, tiled=True),
+        paths_refer(pieces[1]),
         lax.all_gather(pieces[2], "dp", axis=0, tiled=True),
         lax.all_gather(pieces[3], "dp", axis=1, tiled=True),
         lax.all_gather(pieces[4], "dp", axis=0, tiled=True),

time: 1170 us -> 1150 us (0.983)
  blocking collectives: 137 us -> 103 us
  waiting for transfers between devices: 433 us -> 445 us
    all_gather x1 -> x0, blocking collectives: 33.6 us -> none  [on_device(): lax.all_gather(pieces[1], 'dp', axis=1, tiled=True)]
    ppermute x0 -> x3, waiting for transfers between devices: none -> 12.1 us  [build_digits(): ppermute(res, axis_name=named_axis, perm=[(dev, dev ^ x_now) for dev in r...]
  transfers between devices with their start and end apart: 14 -> 17, of which waited for: 10 -> 12; matrix products, arithmetic and copies ran while one was open for 34% -> 34% of each run, Pallas kernels for 0% -> 0%
where the time goes in v1:
time: 1150 us
  waiting for transfers between devices  445 us (39%)
  matrix products  348 us (30%)
  other arithmetic  148 us (13%)
  blocking collectives  103 us (9%)
  local copies, waits for them, and re-layouts  73.3 us (6%)
  between operations  17.8 us (2%)
    convert_element_type x5, other arithmetic, step(): score_grad = (prob * weight_grad - signed * inner).astype(jnp.bfloat16)  76.2 us
    dot_general x5, matrix products, step(): jnp.einsum('qhd,khd->hqk', grad_block, values, preferred_element_type=jnp...  74.7 us
    reduce_scatter x1, waiting for transfers between devices, on_device(): lax.psum_scatter(proj_grad, 'dp', scatter_dimension=1, tiled=True)  73.2 us
    reduce_scatter x1, waiting for transfers between devices, on_device(): lax.psum_scatter(qkv_grad, 'dp', scatter_dimension=0, tiled=True)  73 us
    dot_general x5, matrix products, step(): jnp.einsum('hqk,qhd->khd', rounded, grad_block, preferred_element_type=jn...  69.8 us
    reduce_scatter x1, waiting for transfers between devices, on_device(): lax.psum_scatter(fc_grad, 'dp', scatter_dimension=0, tiled=True)  69.1 us
    unnamed x2, blocking collectives  61 us
    dot_general x5, matrix products, one(): jnp.einsum('hqk,khd->qhd', weights, values, preferred_element_type=jnp.fl...  52.9 us
  transfers between devices with their start and end apart: 17, of which 12 were waited for; matrix products, arithmetic and copies ran while one was open for 34% of the time, Pallas kernels for 0%

profile of v1, /device:TPU:0, one launch (start us, length us, event | category | flops | bytes accessed | tf_op | source)
XLA Modules:
  0.0 1145.5 jit_solution(8026071140519724623)
XLA Ops:
  13.4 23.9 %all-reduce.10 = (bf16[768]{0:T(1024)(128)(2,1)}, bf16[768]{0:T(1024)(128)(2,1)}, bf16[768]{0:T(1024)(128)(2,1)S(1)}, bf16[768]{0:T(1024)(128)(2,1)S(1)}) all-reduce(bf16[768]{0:T(1024)(128)(2,1)S(1)} %dynamic-update-slice.3, bf16[768]{0:T(1024)(128)(2,1)S(1)} %dynamic-update-slice.2, ...), channel_id=1, replica_groups=mesh['dp'=8,'tensor'=4] {'dp'}, use_global_device_ids=true, to_apply=%add.3 | all-reduce | flops 3072 | bytes 12288
  43.5 35.4 %all_gather.36 = bf16[768,3,192]{2,1,0:T(4,128)(2,1)S(1)} all-gather(bf16[96,3,192]{2,1,0:T(4,128)(2,1)S(1)} %copy.33), channel_id=1, replica_groups=mesh['dp'=8,'tensor'=4] {'dp'}, dimensions={0}, use_global_device_ids=true | all-gather | bytes 995328 | tf_op jit(solution)/shard_map/all_gather | solution.py:160
  101.7 122.7 %while.29 = (s32[]{:T(128)}, bf16[5,512,3,64]{1,3,2,0:T(8,128)(2,1)S(1)}, f32[5,3,512]{2,1,0:T(4,128)S(1)}, s32[5]{0:T(128)S(1)}, bf16[2560,3,64]{0,2,1:T(8,128)...) while((s32[]{:T(128)}, ...), condition=%wide.region_7.8_spmd.clone, body=%wide.region_4.7_spmd.clone.sunk | while | flops 1086686208 | bytes 54895824 | solution.py:103
  231.4 39.9 %reduce-scatter.11.cloned.1.call-done = bf16[640,768]{1,0:T(8,128)(2,1)} async-done(((bf16[2560,768]{1,0:T(8,128)(2,1)}), bf16[640,768]{1,0:T(8,128)(2,1)}) %reduce-scatter.11.cloned.1.call-update) | async-done | bytes 983056 | tf_op jit(solution)/shard_map/reduce_scatter | solution.py:189
  276.2 28.8 %all-gather.15.cloned.1.call-done = bf16[2560,768]{1,0:T(8,128)(2,1)} async-done(((bf16[640,768]{1,0:T(8,128)(2,1)}), bf16[2560,768]{1,0:T(8,128)(2,1)}) %all-gather.15.cloned.1.call-update) | async-done | bytes 3932176 | tf_op jit(solution)/shard_map/all_gather | solution.py:209
  313.8 34.7 %all-gather.11.cloned.1.call-done = bf16[768,768]{1,0:T(8,128)(2,1)} async-done(((bf16[96,768]{1,0:T(8,128)(2,1)}), bf16[768,768]{1,0:T(8,128)(2,1)}) %all-gather.11.cloned.1.call-update) | async-done | bytes 1179664 | tf_op jit(solution)/shard_map/all_gather | solution.py:162
  348.4 33.4 %all-gather.9.cloned.1.call-done = bf16[2560,768]{1,0:T(8,128)(2,1)} async-done(((bf16[640,768]{1,0:T(8,128)(2,1)}), bf16[2560,768]{1,0:T(8,128)(2,1)}) %all-gather.9.cloned.1.call-update) | async-done | bytes 3932176 | tf_op jit(solution)/shard_map/all_gather | solution.py:197
  402.4 43.0 %reduce-scatter.15.cloned.1.call-done = bf16[640,768]{1,0:T(8,128)(2,1)} async-done(((bf16[2560,768]{1,0:T(8,128)(2,1)}), bf16[640,768]{1,0:T(8,128)(2,1)}) %reduce-scatter.15.cloned.1.call-update) | async-done | bytes 983056 | tf_op jit(solution)/shard_map/reduce_scatter | solution.py:215
  451.8 32.9 %all-gather.17.cloned.1.call-done = bf16[2560,768]{1,0:T(8,128)(2,1)} async-done(((bf16[640,768]{1,0:T(8,128)(2,1)}), bf16[2560,768]{1,0:T(8,128)(2,1)}) %all-gather.17.cloned.1.call-update) | async-done | bytes 3932176 | tf_op jit(solution)/shard_map/all_gather | solution.py:222
  494.2 323.3 %while.30 = (s32[]{:T(128)}, f32[2560,3,64]{0,2,1:T(8,128)}, f32[2560,3,64]{0,2,1:T(8,128)}, bf16[5,512,3,64]{1,0,3,2:T(8,128)(2,1)}, s32[5]{0:T(128)S(1)}, /*in...) while((s32[]{:T(128)}, f32[2560,3,64]{0,2,1:T(8,128)}, ...), condition=%wide.region_17.18_spmd.clone.clone, body=%wide.region_15.17_spmd.clone.clone.sunk | while | flops 2622784512 | bytes 218457456 | solution.py:145
  513.3 14.9 %multiply_reduce_fusion.3 = (f32[3,512]{1,0:T(4,128)S(1)}, f32[3,512,2560]{2,1,0:T(8,128)}) fusion(f32[3,512,2560]{2,1,0:T(8,128)S(1)} %fusion.137, f32[3,512]{1,0:T(4,128)S(1)} %dynamic-slice_bitcast_fusion.2, pred[512,2560]{1,0:T(8,128)(4,1)S(1)} %or_and_fusion.5, bf16[2560,3,64]{0,2,1:T(8,128)(2,1)S(1)} %copy-done.12, ...), kind=kOutput, calls=%fused_computation.19.clone.1 | convolution fusion | flops 534772224 | bytes 33959940 | tf_op jit(solution)/shard_map/while/body/eval_jaxpr/qhd,khd->hqk/dot_general | solution.py:129
  528.2 15.2 %subtract_convert_fusion.2 = bf16[3,512,2560]{2,1,0:T(8,128)(2,1)S(1)} fusion(f32[3,512,2560]{2,1,0:T(8,128)} %get-tuple-element.439, f32[3,512,2560]{2,1,0:T(8,128)} %copy-done, f32[3,512]{1,0:T(4,128)S(1)} %get-tuple-element.440, f32[3,512]{1,0:T(4,128)S(1)} %dynamic-slice_bitcast_fusion.2, pred[512,2560]{1,0:T(8,128)(4,1)S(1)} %or_and_fusion.5), kind=kLoop, calls=%fused_computation.18.clone.1 | loop fusion | flops 39321600 | bytes 40644608 | tf_op jit(solution)/shard_map/while/body/eval_jaxpr/convert_element_type | solution.py:133
  578.3 14.9 %multiply_reduce_fusion.3 = (f32[3,512]{1,0:T(4,128)S(1)}, f32[3,512,2560]{2,1,0:T(8,128)}) fusion(f32[3,512,2560]{2,1,0:T(8,128)S(1)} %fusion.137, f32[3,512]{1,0:T(4,128)S(1)} %dynamic-slice_bitcast_fusion.2, pred[512,2560]{1,0:T(8,128)(4,1)S(1)} %or_and_fusion.5, bf16[2560,3,64]{0,2,1:T(8,128)(2,1)S(1)} %copy-done.12, ...), kind=kOutput, calls=%fused_computation.19.clone.1 | convolution fusion | flops 534772224 | bytes 33959940 | tf_op jit(solution)/shard_map/while/body/eval_jaxpr/qhd,khd->hqk/dot_general | solution.py:129
  593.2 15.2 %subtract_convert_fusion.2 = bf16[3,512,2560]{2,1,0:T(8,128)(2,1)S(1)} fusion(f32[3,512,2560]{2,1,0:T(8,128)} %get-tuple-element.439, f32[3,512,2560]{2,1,0:T(8,128)} %copy-done, f32[3,512]{1,0:T(4,128)S(1)} %get-tuple-element.440, f32[3,512]{1,0:T(4,128)S(1)} %dynamic-slice_bitcast_fusion.2, pred[512,2560]{1,0:T(8,128)(4,1)S(1)} %or_and_fusion.5), kind=kLoop, calls=%fused_computation.18.clone.1 | loop fusion | flops 39321600 | bytes 40644608 | tf_op jit(solution)/shard_map/while/body/eval_jaxpr/convert_element_type | solution.py:133
  643.2 14.9 %multiply_reduce_fusion.3 = (f32[3,512]{1,0:T(4,128)S(1)}, f32[3,512,2560]{2,1,0:T(8,128)}) fusion(f32[3,512,2560]{2,1,0:T(8,128)S(1)} %fusion.137, f32[3,512]{1,0:T(4,128)S(1)} %dynamic-slice_bitcast_fusion.2, pred[512,2560]{1,0:T(8,128)(4,1)S(1)} %or_and_fusion.5, bf16[2560,3,64]{0,2,1:T(8,128)(2,1)S(1)} %copy-done.12, ...), kind=kOutput, calls=%fused_computation.19.clone.1 | convolution fusion | flops 534772224 | bytes 33959940 | tf_op jit(solution)/shard_map/while/body/eval_jaxpr/qhd,khd->hqk/dot_general | solution.py:129
  658.2 15.2 %subtract_convert_fusion.2 = bf16[3,512,2560]{2,1,0:T(8,128)(2,1)S(1)} fusion(f32[3,512,2560]{2,1,0:T(8,128)} %get-tuple-element.439, f32[3,512,2560]{2,1,0:T(8,128)} %copy-done, f32[3,512]{1,0:T(4,128)S(1)} %get-tuple-element.440, f32[3,512]{1,0:T(4,128)S(1)} %dynamic-slice_bitcast_fusion.2, pred[512,2560]{1,0:T(8,128)(4,1)S(1)} %or_and_fusion.5), kind=kLoop, calls=%fused_computation.18.clone.1 | loop fusion | flops 39321600 | bytes 40644608 | tf_op jit(solution)/shard_map/while/body/eval_jaxpr/convert_element_type | solution.py:133
  708.2 14.9 %multiply_reduce_fusion.3 = (f32[3,512]{1,0:T(4,128)S(1)}, f32[3,512,2560]{2,1,0:T(8,128)}) fusion(f32[3,512,2560]{2,1,0:T(8,128)S(1)} %fusion.137, f32[3,512]{1,0:T(4,128)S(1)} %dynamic-slice_bitcast_fusion.2, pred[512,2560]{1,0:T(8,128)(4,1)S(1)} %or_and_fusion.5, bf16[2560,3,64]{0,2,1:T(8,128)(2,1)S(1)} %copy-done.12, ...), kind=kOutput, calls=%fused_computation.19.clone.1 | convolution fusion | flops 534772224 | bytes 33959940 | tf_op jit(solution)/shard_map/while/body/eval_jaxpr/qhd,khd->hqk/dot_general | solution.py:129
  723.2 15.2 %subtract_convert_fusion.2 = bf16[3,512,2560]{2,1,0:T(8,128)(2,1)S(1)} fusion(f32[3,512,2560]{2,1,0:T(8,128)} %get-tuple-element.439, f32[3,512,2560]{2,1,0:T(8,128)} %copy-done, f32[3,512]{1,0:T(4,128)S(1)} %get-tuple-element.440, f32[3,512]{1,0:T(4,128)S(1)} %dynamic-slice_bitcast_fusion.2, pred[512,2560]{1,0:T(8,128)(4,1)S(1)} %or_and_fusion.5), kind=kLoop, calls=%fused_computation.18.clone.1 | loop fusion | flops 39321600 | bytes 40644608 | tf_op jit(solution)/shard_map/while/body/eval_jaxpr/convert_element_type | solution.py:133
  773.2 14.9 %multiply_reduce_fusion.3 = (f32[3,512]{1,0:T(4,128)S(1)}, f32[3,512,2560]{2,1,0:T(8,128)}) fusion(f32[3,512,2560]{2,1,0:T(8,128)S(1)} %fusion.137, f32[3,512]{1,0:T(4,128)S(1)} %dynamic-slice_bitcast_fusion.2, pred[512,2560]{1,0:T(8,128)(4,1)S(1)} %or_and_fusion.5, bf16[2560,3,64]{0,2,1:T(8,128)(2,1)S(1)} %copy-done.12, ...), kind=kOutput, calls=%fused_computation.19.clone.1 | convolution fusion | flops 534772224 | bytes 33959940 | tf_op jit(solution)/shard_map/while/body/eval_jaxpr/qhd,khd->hqk/dot_general | solution.py:129
  788.1 15.2 %subtract_convert_fusion.2 = bf16[3,512,2560]{2,1,0:T(8,128)(2,1)S(1)} fusion(f32[3,512,2560]{2,1,0:T(8,128)} %get-tuple-element.439, f32[3,512,2560]{2,1,0:T(8,128)} %copy-done, f32[3,512]{1,0:T(4,128)S(1)} %get-tuple-element.440, f32[3,512]{1,0:T(4,128)S(1)} %dynamic-slice_bitcast_fusion.2, pred[512,2560]{1,0:T(8,128)(4,1)S(1)} %or_and_fusion.5), kind=kLoop, calls=%fused_computation.18.clone.1 | loop fusion | flops 39321600 | bytes 40644608 | tf_op jit(solution)/shard_map/while/body/eval_jaxpr/convert_element_type | solution.py:133
  874.6 37.1 %all-reduce.8 = (f32[768]{0:T(1024)S(1)}, f32[768]{0:T(1024)S(1)}, f32[768]{0:T(1024)S(1)}, f32[768]{0:T(1024)S(1)}) all-reduce(f32[768]{0:T(1024)S(1)} %get-tuple-element.224, f32[768]{0:T(1024)S(1)} %get-tuple-element.229, f32[768]{0:T(1024)S(1)} %copy-done.34, ...), channel_id=10, replica_groups=mesh['dp'=8,'tensor'=4] {'dp'}, use_global_device_ids=true, to_apply=%region_26.27.clone | all-reduce | flops 3072 | bytes 24576
  922.6 69.1 %reduce-scatter.21.cloned.1.call-done = f32[96,768]{1,0:T(8,128)} async-done(((f32[768,768]{1,0:T(8,128)}), f32[96,768]{1,0:T(8,128)}) %reduce-scatter.21.cloned.1.call-update) | async-done | bytes 294928 | tf_op jit(solution)/shard_map/reduce_scatter | solution.py:244
  991.7 73.2 %reduce-scatter.23.cloned.1.call-done = f32[768,96]{0,1:T(8,128)} async-done(((f32[768,768]{0,1:T(8,128)}), f32[768,96]{0,1:T(8,128)}) %reduce-scatter.23.cloned.1.call-update) | async-done | bytes 294928 | tf_op jit(solution)/shard_map/reduce_scatter | solution.py:245
  1065.0 73.0 %reduce-scatter.19.cloned.1.call-done = f32[96,3,192]{2,0,1:T(8,128)} async-done(((f32[768,3,192]{2,0,1:T(8,128)}), f32[96,3,192]{2,0,1:T(8,128)}) %reduce-scatter.19.cloned.1.call-update) | async-done | bytes 221200 | tf_op jit(solution)/shard_map/reduce_scatter | solution.py:242
  (336 shorter events, 443.9 us)
Async XLA Ops:
  8.0 87.7 %all-gather.7.cloned.1.call-start = ((), (), s32[]{:S(2)}) async-start(), calls=%async_computation.8 | async-start | bytes 4915200 | tf_op jit(solution)/shard_map/all_gather | solution.py:181
  43.0 228.2 %reduce-scatter.11.cloned.1.call-start = ((), (), s32[]{:S(2)}) async-start(), calls=%async_computation.9 | async-start | bytes 4915200 | tf_op jit(solution)/shard_map/reduce_scatter | solution.py:189
  43.1 37.9 %collective-permute-start = (bf16[1,192,96]{2,1,0:T(8,128)(2,1)S(1)}, bf16[1,192,96]{2,1,0:T(8,128)(2,1)S(1)}, u32[]{:S(2)}, u32[]{:S(2)}) collective-permute-start(bf16[1,192,96]{2,1,0:T(8,128)(2,1)S(1)} %bitcast.132), channel_id=1, source_target_pairs={{0,4},{4,0},{8,12},{12,8},{16,20},{20,16},{24,28},{28,24},{1,5},{5... | collective-permute-start | bytes 110600 | tf_op jit(solution)/shard_map/ppermute | solution.py:22
  81.1 5.1 collective-permute-start.1
  86.2 8.0 collective-permute-start.2
  229.6 46.6 %all-gather.13.cloned.1.call-start = ((), (), s32[]{:S(2)}) async-start(), calls=%async_computation.12 | async-start | bytes 1327104 | tf_op jit(solution)/shard_map/all_gather | solution.py:163
  230.1 74.8 %all-gather.15.cloned.1.call-start = ((), (), s32[]{:S(2)}) async-start(), calls=%async_computation.14 | async-start | bytes 4915200 | tf_op jit(solution)/shard_map/all_gather | solution.py:209
  230.7 117.7 %all-gather.11.cloned.1.call-start = ((), (), s32[]{:S(2)}) async-start(), calls=%async_computation.11 | async-start | bytes 1327104 | tf_op jit(solution)/shard_map/all_gather | solution.py:162
  231.3 150.5 %all-gather.9.cloned.1.call-start = ((), (), s32[]{:S(2)}) async-start(), calls=%async_computation.10 | async-start | bytes 4915200 | tf_op jit(solution)/shard_map/all_gather | solution.py:197
  231.4 216.9 %copy-start.21 = (f32[768]{0:T(1024)}, f32[768]{0:T(1024)S(1)}, u32[]{:S(2)}) copy-start(f32[768]{0:T(1024)S(1)} %convert_element_type.109) | copy-start | bytes 9220
  272.9 175.4 %copy-start.17 = (f32[640]{0:T(1024)}, f32[640]{0:T(1024)S(1)}, u32[]{:S(2)}) copy-start(f32[640]{0:T(1024)S(1)} %broadcast_multiply_fusion.4) | copy-start | bytes 7684
  274.6 173.7 %copy-start.23 = (f32[640]{0:T(1024)}, f32[640]{0:T(1024)S(1)}, u32[]{:S(2)}) copy-start(f32[640]{0:T(1024)S(1)} %add_rsqrt_fusion) | copy-start | bytes 7684
  276.1 169.3 %reduce-scatter.15.cloned.1.call-start = ((), (), s32[]{:S(2)}) async-start(), calls=%async_computation.15 | async-start | bytes 4915200 | tf_op jit(solution)/shard_map/reduce_scatter | solution.py:215
  402.4 82.3 %all-gather.17.cloned.1.call-start = ((), (), s32[]{:S(2)}) async-start(), calls=%async_computation.16 | async-start | bytes 4915200 | tf_op jit(solution)/shard_map/all_gather | solution.py:222
  451.7 415.7 %reduce-scatter.25.cloned.1.call-start = ((), (), s32[]{:S(2)}) async-start(), calls=%async_computation.21 | async-start | bytes 884736
  489.7 382.7 %reduce-scatter.17.cloned.1.call-start = ((), (), s32[]{:S(2)}) async-start(), calls=%async_computation.17 | async-start | bytes 4915200 | tf_op jit(solution)/shard_map/reduce_scatter | solution.py:235
  829.5 88.9 %reduce-scatter.13.cloned.1.call-start = ((), (), s32[]{:S(2)}) async-start(), calls=%async_computation.13 | async-start | bytes 4915200 | tf_op jit(solution)/shard_map/reduce_scatter | solution.py:202
  840.7 151.0 %reduce-scatter.21.cloned.1.call-start = ((), (), s32[]{:S(2)}) async-start(), calls=%async_computation.19 | async-start | bytes 2654208 | tf_op jit(solution)/shard_map/reduce_scatter | solution.py:244
  848.9 216.1 %reduce-scatter.23.cloned.1.call-start = ((), (), s32[]{:S(2)}) async-start(), calls=%async_computation.20 | async-start | bytes 2654208 | tf_op jit(solution)/shard_map/reduce_scatter | solution.py:245
  858.8 279.2 %reduce-scatter.19.cloned.1.call-start = ((), (), s32[]{:S(2)}) async-start(), calls=%async_computation.18 | async-start | bytes 2654208 | tf_op jit(solution)/shard_map/reduce_scatter | solution.py:242
  866.6 51.8 %copy-start.18 = (f32[640]{0:T(1024)S(1)}, f32[640]{0:T(1024)}, u32[]{:S(2)}) copy-start(f32[640]{0:T(1024)} %copy-done.17) | copy-start | bytes 7684
  866.6 51.8 %copy-start.22 = (f32[768]{0:T(1024)S(1)}, f32[768]{0:T(1024)}, u32[]{:S(2)}) copy-start(f32[768]{0:T(1024)} %copy-done.21) | copy-start | bytes 9220
  866.6 51.8 %copy-start.24 = (f32[640]{0:T(1024)S(1)}, f32[640]{0:T(1024)}, u32[]{:S(2)}) copy-start(f32[640]{0:T(1024)} %copy-done.23) | copy-start | bytes 7684
  866.6 51.8 %copy-start.31 = (f32[640]{0:T(1024)S(1)}, f32[640]{0:T(1024)}, u32[]{:S(2)}) copy-start(f32[640]{0:T(1024)} %copy-done.30) | copy-start | bytes 7684
  (51 other events, 717.8 us)
Sparse Core Ops, SparseCore 0:
  43.2 30.2 all-gather.6
  229.7 41.5 reduce-scatter.10
  402.5 42.9 reduce-scatter.14
Sparse Core Ops, SparseCore 1:
  232.2 40.0 all-gather.12
  273.7 31.2 all-gather.14
  307.0 41.4 all-gather.10
  350.6 31.2 all-gather.8
  451.8 32.8 all-gather.16
  489.7 63.3 reduce-scatter.24
  829.6 42.7 reduce-scatter.16
  874.8 42.8 reduce-scatter.12
  921.6 70.1 reduce-scatter.20
  995.8 69.1 reduce-scatter.22
  1068.9 69.0 reduce-scatter.18
